TPU v7x, 32 devices: a whole 2x2x4 slice. The times are simulated.
32 devices in a mesh: ang: 16 (over z, y, x), slab: 2 (over core).
Axes of the slice: x: 2, y: 2, z: 4, core: 2. Of those that a mesh axis runs over, the one named last changes fastest.
Arguments:
- updates: float32 [64, 2, 256, 512], P('ang', None, 'slab'), may hold values from -6 to 6
- interp_tiles: bfloat16 [64, 32, 256, 128], P('ang'), may hold values from -0.1875 to 0.1875
- band_start: int32 [64, 32], P('ang'), may hold values from 0 to 2
- angle_id: int32 [64], P('ang'), may hold values from 0 to 63, each once
- angle_weight: float32 [64], replicated, may hold values from 0.05 to 0.5
- volume: float32 [4096, 2, 256], P('ang', None, 'slab'), may hold values from -6 to 6
Outputs:
- volume_next: float32 [4096, 2, 256], P('ang', None, 'slab')
- projection: float32 [64, 2, 256, 512], P('ang', None, 'slab')
Inputs may be any that keep to these rules, and one draw needn't show every extreme that they name: Tile j of angle slot a reads detector columns 128 * band_start[a, j] up to 256 further. `angle_id`: each measured angle stands in exactly one slot.
All inputs are finite; a program needn't handle non-finite values.
Results may differ from a plain program's by a relative error of at most 0.0062.
Values may be sent and summed in bfloat16 or wider, within the bound.
A program may use at most 128 MiB of HBM per device.

v0:
```python
import jax
import jax.numpy as jnp
from jax import lax
from jax.sharding import PartitionSpec as P

SMOOTHING = 0.25


def extended(cells, sides, width):
    for axis, dim in sides:
        count = lax.axis_size(axis)
        ends = count - 1
        head = lax.slice_in_dim(cells, 0, width, axis=dim)
        tail = lax.slice_in_dim(cells, cells.shape[dim] - width, cells.shape[dim], axis=dim)
        cells = jnp.concatenate(
            [
                lax.ppermute(tail, axis, [(i, (i + 1) % count) for i in range(ends)]),
                cells,
                lax.ppermute(head, axis, [((i + 1) % count, i) for i in range(ends)]),
            ],
            axis=dim,
        )
    return cells


def clamp_absorption(field):
    channel = jnp.arange(2, dtype=jnp.int32)[None, :, None]
    return jnp.where(channel == 1, jnp.maximum(field, 0.0), field)


def shards(updates, interp_tiles, band_start, angle_id, angle_weight, volume):
    local_angles = updates.shape[0]
    slab_depth = updates.shape[2]
    detector = updates.shape[3]
    band_width = interp_tiles.shape[2]
    block_size = interp_tiles.shape[3]
    row_count = 2 * slab_depth
    position_count = detector // block_size - 1
    share = volume.shape[0]
    matches = angle_id[:, None] == jnp.arange(angle_weight.shape[0], dtype=jnp.int32)[None, :]
    chosen = jnp.sum(jnp.where(matches, angle_weight[None, :], 0.0), axis=1)
    scaled = (
        (chosen[:, None, None, None] * updates)
        .astype(jnp.bfloat16)
        .reshape(local_angles, row_count, detector)
    )
    stacked = jnp.stack(
        [
            lax.slice_in_dim(
                scaled, block_size * offset_index, block_size * offset_index + band_width, axis=2
            )
            for offset_index in range(position_count)
        ],
        axis=1,
    )
    positions = jnp.arange(position_count, dtype=jnp.int32)
    padded = extended(volume, (("slab", 2),), 1)
    smooth = volume - SMOOTHING * (2.0 * volume - padded[:, :, :-2] - padded[:, :, 2:])
    tile_part = interp_tiles
    start_part = band_start
    onehot = (start_part[:, :, None] == positions).astype(jnp.bfloat16)
    windows = jnp.einsum(
        "ajk,akrq->ajrq", onehot, stacked, preferred_element_type=jnp.float32
    ).astype(jnp.bfloat16)
    term = jnp.einsum("ajrq,ajqp->jpr", windows, tile_part, preferred_element_type=jnp.float32)
    summed = lax.psum_scatter(
        term.reshape(share * lax.axis_size("ang"), 2, slab_depth),
        "ang",
        scatter_dimension=0,
        tiled=True,
    )
    volume_next = clamp_absorption(smooth + summed)
    piece = lax.all_gather(volume_next.astype(jnp.bfloat16), "ang", axis=0, tiled=True)
    tile_count = piece.shape[0] // block_size
    tile_part = interp_tiles
    start_part = band_start
    images = jnp.einsum(
        "jpr,ajqp->ajrq",
        piece.reshape(tile_count, block_size, row_count),
        tile_part,
        preferred_element_type=jnp.float32,
    )
    onehot = (start_part[:, :, None] == positions).astype(jnp.float32)
    grouped = jnp.einsum("ajk,ajrq->akrq", onehot, images, precision=lax.Precision.HIGHEST)
    projection = jnp.zeros((local_angles, row_count, detector), jnp.float32)
    for offset_index in range(position_count):
        projection = projection + jnp.pad(
            grouped[:, offset_index],
            (
                (0, 0),
                (0, 0),
                (block_size * offset_index, detector - block_size * offset_index - band_width),
            ),
        )
    return (volume_next, projection.reshape(local_angles, 2, slab_depth, detector))


def solution(mesh):
    placed = (
        P("ang", None, "slab", None),
        P("ang", None, None, None),
        P("ang", None),
        P("ang"),
        P(),
        P("ang", None, "slab"),
    )
    return jax.shard_map(
        shards,
        mesh=mesh,
        in_specs=placed,
        out_specs=(P("ang", None, "slab"), P("ang", None, "slab", None)),
        check_vma=False,
    )
```

profile of v0, /device:TPU:0, one launch (start us, length us, event | category | flops | bytes accessed | tf_op | source)
XLA Modules:
  0.0 299.1 jit_solution(14533602064375332283)
XLA Ops:
  7.2 0.0 reduce-scatter.2.cloned.1.call-start
  7.2 0.9 select_reduce_fusion
  8.1 1.9 multiply_convert_fusion
  10.0 0.0 copy-start.1
  10.0 0.1 slice_bitcast_fusion.2
  10.1 0.8 copy.78
  11.0 0.8 copy.80
  11.8 0.0 slice-start
  11.8 0.8 copy.79
  12.6 0.0 copy-done.1
  12.6 0.0 slice-start.1
  12.6 9.1 %convolution_convert_fusion = bf16[4,32,256,256]{3,1,2,0:T(8,128)(2,1)} fusion(bf16[4,1,256,256]{3,1,2,0:T(2,128)(2,1)S(1)} %copy.80, bf16[4,1,256,256]{3,1,2,0:T(2,128)(2,1)S(1)} %copy.79, bf16[4,1,256,256]{3,1,2,0:T(2,128)(2,1)S(1)} %copy.78, s32[4,32]{1,0:T(4,128)S(1)} %copy-done.1), kind=kOutput, calls=%fused_computation.5 | convolution fusion | flops 63439232 | bytes 18350592 | tf_op jit(solution)/shard_map/ajk,akrq->ajrq/dot_general | solution.py:62
  21.8 0.0 slice-done
  21.8 0.0 slice-done.1
  21.8 21.9 %fusion.6 = f32[32,128,256]{1,2,0:T(8,128)} fusion(bf16[4,32,256,128]{3,2,1,0:T(8,128)(2,1)S(1)} %bitcast.38, bf16[4,32,256,256]{3,1,2,0:T(8,128)(2,1)} %convolution_convert_fusion), kind=kOutput, calls=%fused_computation.8 | convolution fusion | flops 2147483648 | bytes 29360128 | tf_op jit(solution)/shard_map/ajrq,ajqp->jpr/dot_general | solution.py:65
  43.6 6.6 %copy.83 = f32[32,128,256]{1,0,2:T(8,128)} copy(f32[32,128,256]{1,2,0:T(8,128)} %fusion.6) | data formatting | bytes 8388608 | tf_op jit(solution)/shard_map/ajrq,ajqp->jpr/dot_general | solution.py:65
  50.2 5.0 %reshape.26 = f32[4096,2,128]{0,2,1:T(8,128)} reshape(f32[32,128,256]{1,0,2:T(8,128)} %copy.83) | data formatting | bytes 8388608 | tf_op jit(solution)/shard_map/reshape | solution.py:67
  55.2 0.0 copy-start
  55.2 0.0 reduce-scatter.2.cloned.1.call-update
  55.2 0.0 all-gather.2.cloned.1.call-start
  55.3 0.9 copy-done
  56.1 0.1 copy.77
  56.3 2.4 collective-permute-start
  58.7 1.3 collective-permute-start.1
  60.0 0.0 collective-permute-done
  60.0 1.7 collective-permute-done.1
  61.8 91.6 %reduce-scatter.2.cloned.1.call-done = f32[256,2,128]{0,2,1:T(8,128)} async-done(((f32[4096,2,128]{0,2,1:T(8,128)}), f32[256,2,128]{0,2,1:T(8,128)}) %reduce-scatter.2.cloned.1.call-update) | async-done | bytes 262160 | tf_op jit(solution)/shard_map/reduce_scatter | solution.py:66
  153.3 1.7 fusion.28
  155.1 0.0 all-gather.2.cloned.1.call-update
  155.1 0.8 copy.89
  155.9 65.0 %all-gather.2.cloned.1.call-done = bf16[4096,2,128]{0,2,1:T(8,128)(2,1)} async-done(((bf16[256,2,128]{0,2,1:T(8,128)(2,1)}), bf16[4096,2,128]{0,2,1:T(8,128)(2,1)}) %all-gather.2.cloned.1.call-update) | async-done | bytes 2097168 | tf_op jit(solution)/shard_map/all_gather | solution.py:73
  220.9 2.1 copy.98
  223.0 19.0 %convolution_bitcast_fusion = f32[4,32,256,256]{3,2,0,1:T(8,128)} fusion(bf16[4,32,256,128]{3,2,1,0:T(8,128)(2,1)} %param.7, bf16[32,128,256,1]{1,0,2,3:T(8,128)(2,1)S(1)} %bitcast.39), kind=kOutput, calls=%fused_computation.4 | convolution fusion | flops 2147483648 | bytes 44040192 | tf_op jit(solution)/shard_map/jpr,ajqp->ajrq/dot_general | solution.py:77
  241.9 40.4 %fusion = f32[4,3,256,256]{3,1,2,0:T(4,128)} fusion(f32[4,32,256,256]{3,2,0,1:T(8,128)} %convolution_bitcast_fusion, s32[4,32]{1,0:T(4,128)S(1)} %copy-done.1), kind=kOutput, calls=%fused_computation | convolution fusion | flops 301990272 | bytes 36700672 | tf_op jit(solution)/shard_map/ajk,ajrq->akrq/dot_general | solution.py:84
  282.4 7.5 %fusion.29 = (f32[4,1,256,256]{3,1,2,0:T(1,128)S(1)}, f32[4,1,256,256]{3,1,2,0:T(1,128)S(1)}, f32[4,1,256,256]{3,1,2,0:T(1,128)S(1)}) fusion(f32[4,3,256,256]{3,1,2,0:T(4,128)} %fusion), kind=kLoop, calls=%fused_computation.40 | loop fusion | bytes 6291456 | tf_op jit(solution)/shard_map/slice | solution.py:88
  289.9 0.1 copy.116
  290.0 0.2 copy_bitcast_fusion
  290.2 1.6 pad_add_fusion
  (3 shorter events, 0.0 us)
Async XLA Ops:
  7.2 146.2 %reduce-scatter.2.cloned.1.call-start = ((), (), s32[]{:S(2)}) async-start(), calls=%async_computation.1 | async-start | bytes 4456448 | tf_op jit(solution)/shard_map/reduce_scatter | solution.py:66
  10.0 2.6 copy-start.1
  11.8 10.0 %slice-start = ((s8[8388608]{0:T(1024)(128)(4,1)}), s8[4194304]{0:T(1024)(128)(4,1)S(1)}, s32[]{:S(2)}) async-start(s8[8388608]{0:T(1024)(128)(4,1)} %bitcast.37), calls=%async_computation.3 | async-start | bytes 8388608
  12.6 9.1 %slice-start.1 = ((s8[8388608]{0:T(1024)(128)(4,1)}), s8[4194304]{0:T(1024)(128)(4,1)S(1)}, s32[]{:S(2)}) async-start(s8[8388608]{0:T(1024)(128)(4,1)} %bitcast.37), calls=%async_computation.4 | async-start | bytes 8388608
  55.2 0.9 copy-start
  55.2 165.7 %all-gather.2.cloned.1.call-start = ((), (), s32[]{:S(2)}) async-start(), calls=%async_computation.2 | async-start | bytes 2228224 | tf_op jit(solution)/shard_map/all_gather | solution.py:73
  56.3 3.7 %collective-permute-start = (f32[256,2,1]{0,2,1:T(1,128)S(1)}, f32[256,2,1]{0,2,1:T(1,128)S(1)}, u32[]{:S(2)}, u32[]{:S(2)}) collective-permute-start(f32[256,2,1]{0,2,1:T(1,128)S(1)} %get-tuple-element.20), channel_id=1, source_target_pairs={{0,1},{2,3},{4,5},{6,7},{8,9},{10,11},{12,13},{14,15},{16,17},{18,... | collective-permute-start | bytes 6152 | tf_op jit(solution)/shard_map/ppermute | solution.py:17
  58.7 3.1 %collective-permute-start.1 = (f32[256,2,1]{0,2,1:T(1,128)S(1)}, f32[256,2,1]{0,2,1:T(1,128)S(1)}, u32[]{:S(2)}, u32[]{:S(2)}) collective-permute-start(f32[256,2,1]{0,2,1:T(1,128)S(1)} %get-tuple-element.21), channel_id=1, source_target_pairs={{1,0},{3,2},{5,4},{7,6},{9,8},{11,10},{13,12},{15,14},{17,16},{19,... | collective-permute-start | bytes 6152 | tf_op jit(solution)/shard_map/ppermute | solution.py:19
Sparse Core Ops, SparseCore 0:
  55.3 97.9 reduce-scatter.1
  156.6 64.2 all-gather.1
where the time goes:
time: 302 us; the launch traced here: 299 us
  waiting for transfers between devices  158 us (52%)
  matrix products  90.4 us (30%)
  local copies, waits for them, and re-layouts  25.9 us (9%)
  between operations  14.6 us (5%)
  other arithmetic  6.12 us (2%)
  starting transfers between devices  3.77 us (1%)
    reduce_scatter x1, waiting for transfers between devices, shards(): lax.psum_scatter(term.reshape(share * lax.axis_size('ang'), 2, slab_depth...  91.6 us
    all_gather x1, waiting for transfers between devices, shards(): lax.all_gather(volume_next.astype(jnp.bfloat16), 'ang', axis=0, tiled=True)  65 us
    dot_general x1, matrix products, shards(): jnp.einsum('ajk,ajrq->akrq', onehot, images, precision=lax.Precision.HIGH...  40.4 us
    dot_general x1, matrix products, shards(): jnp.einsum('ajrq,ajqp->jpr', windows, tile_part, preferred_element_type=j...  21.9 us
    dot_general x1, matrix products, shards(): jnp.einsum('jpr,ajqp->ajrq', piece.reshape(tile_count, block_size, row_co...  19 us
    dot_general x1, matrix products, shards(): jnp.einsum('ajk,akrq->ajrq', onehot, stacked, preferred_element_type=jnp....  9.13 us
    slice x1, local copies, waits for them, and re-layouts, shards(): grouped[:, offset_index]  7.52 us
    dot_general x1, local copies, waits for them, and re-layouts, shards(): jnp.einsum('ajrq,ajqp->jpr', windows, tile_part, preferred_element_type=j...  6.56 us
  transfers between devices with their start and end apart: 4, of which 3 were waited for; matrix products, arithmetic and copies ran while one was open for 0% of the time, Pallas kernels for 0%

commit v1 on v0

v1 whole, which is shorter than its diff:
```python
import functools

import jax
import jax.numpy as jnp
from jax import lax
from jax.experimental import pallas as pl
from jax.experimental.pallas import tpu as pltpu
from jax.sharding import PartitionSpec as P

SMOOTHING = 0.25
MESH = pl.DeviceIdType.MESH


def kernel(
    groups,
    slabs,
    turns,
    starts_ref,
    ids_ref,
    weights_ref,
    updates_ref,
    tiles_hbm,
    volume_ref,
    next_ref,
    projection_ref,
    tiles_ref,
    wide_ref,
    scaled_ref,
    sent_ref,
    landed_ref,
    gathered_ref,
    halo_ref,
    tile_sems,
    send_sem,
    land_sems,
    spread_sem,
    gather_sems,
    halo_sems,
):
    local_angles, row_count, detector = updates_ref.shape
    tile_count, band_width, block_size = tiles_ref.shape[1:]
    share = sent_ref.shape[2]
    unit = wide_ref.shape[2]
    unit_count = wide_ref.shape[0]
    per_unit = unit // share
    unit_tiles = unit // block_size
    depth = row_count // 2
    column_blocks = detector // block_size
    halves = band_width // block_size
    me = lax.axis_index("ang")
    slab = lax.axis_index("slab")
    my_unit = me // per_unit

    def unit_at(step):
        return lax.rem(my_unit + step, unit_count)

    def tile_copy(where):
        block = pl.ds(where * unit_tiles, unit_tiles)
        return pltpu.make_async_copy(
            tiles_hbm.at[:, block], tiles_ref.at[:, block], tile_sems.at[where]
        )

    @pl.loop(1, unit_count + 1)
    def _(step):
        tile_copy(unit_at(step)).start()

    barrier = pltpu.get_barrier_semaphore()

    @pl.loop(1, groups)
    def _(step):
        peer = lax.rem(me + step, groups)
        pl.semaphore_signal(barrier, inc=1, device_id=(peer, slab), device_id_type=MESH)

    for turn in turns:
        beside = lax.rem(slab + turn, slabs)
        pl.semaphore_signal(barrier, inc=1, device_id=(me, beside), device_id_type=MESH)

    for angle in range(local_angles):
        chosen = weights_ref[ids_ref[angle]]
        scaled_ref[:, angle * detector : (angle + 1) * detector] = (
            chosen * updates_ref[angle]
        ).astype(jnp.bfloat16)

    pl.semaphore_wait(barrier, groups - 1 + len(turns))

    halo_copies = []
    for slot, turn in enumerate(turns):
        halo_copies.append(
            pltpu.make_async_remote_copy(
                src_ref=volume_ref,
                dst_ref=halo_ref.at[slot],
                send_sem=halo_sems.at[0, slot],
                recv_sem=halo_sems.at[1, slot],
                device_id=(me, lax.rem(slab + turn, slabs)),
                device_id_type=MESH,
            )
        )
        halo_copies[-1].start()

    def term_copy(owner):
        return pltpu.make_async_remote_copy(
            src_ref=sent_ref.at[owner],
            dst_ref=landed_ref.at[me],
            send_sem=send_sem.at[owner],
            recv_sem=land_sems.at[me],
            device_id=(owner, slab),
            device_id_type=MESH,
        )

    def back(where):
        tile_copy(where).wait()
        for angle in range(local_angles):
            for part in range(unit_tiles):
                index = where * unit_tiles + part
                first = starts_ref[angle, index]
                for column in range(column_blocks):
                    block = jnp.zeros((block_size, block_size), jnp.bfloat16)
                    for half in range(halves):
                        held = tiles_ref[
                            angle, index, half * block_size : (half + 1) * block_size, :
                        ]
                        block = jnp.where(first + half == column, held, block)
                    top = angle * detector + column * block_size
                    wide_ref[
                        where,
                        top : top + block_size,
                        part * block_size : (part + 1) * block_size,
                    ] = block
        term = jnp.dot(
            scaled_ref[...], wide_ref[where], preferred_element_type=jnp.float32
        ).astype(jnp.bfloat16)
        for part in range(per_unit):
            sent_ref[where * per_unit + part] = term[:, part * share : (part + 1) * share]

    @pl.loop(1, unit_count)
    def _(step):
        where = unit_at(step)
        back(where)
        for part in range(per_unit):
            term_copy(where * per_unit + part).start()

    back(my_unit)
    if per_unit > 1:
        for part in range(per_unit):
            owner = my_unit * per_unit + part

            @pl.when(owner != me)
            def _():
                term_copy(owner).start()

    landed_ref[me] = sent_ref[me]

    def land_wait(step):
        source = lax.rem(me + groups - step, groups)
        pltpu.make_async_remote_copy(
            src_ref=sent_ref.at[source],
            dst_ref=landed_ref.at[source],
            send_sem=send_sem.at[source],
            recv_sem=land_sems.at[source],
            device_id=(source, slab),
            device_id_type=MESH,
        ).wait_recv()

    pl.loop(1, groups)(land_wait)
    for halo_copy in halo_copies:
        halo_copy.wait()

    lane = lax.broadcasted_iota(jnp.int32, (share, depth), 1)
    for channel in range(2):
        rows = slice(channel * depth, (channel + 1) * depth)
        total = lax.fori_loop(
            1,
            groups,
            lambda i, acc: acc + landed_ref[i, rows, :].astype(jnp.float32),
            landed_ref[0, rows, :].astype(jnp.float32),
        )
        if share % 128:
            room = 128 - share % 128
            total = jnp.concatenate([total, jnp.zeros((depth, room), jnp.float32)], axis=1)
        total = total.T[:share]
        cells = volume_ref[:, channel, :]
        before = pltpu.roll(cells, 1, 1)
        after = pltpu.roll(cells, depth - 1, 1)
        edge_before = jnp.zeros_like(cells)
        edge_after = jnp.zeros_like(cells)
        if slabs > 1:
            lower = halo_ref[0, :, channel, :]
            upper = halo_ref[len(turns) - 1, :, channel, :]
            edge_before = jnp.where(slab > 0, pltpu.roll(lower, 1, 1), edge_before)
            edge_after = jnp.where(
                slab < slabs - 1, pltpu.roll(upper, depth - 1, 1), edge_after
            )
        before = jnp.where(lane == 0, edge_before, before)
        after = jnp.where(lane == depth - 1, edge_after, after)
        smooth = cells - SMOOTHING * (2.0 * cells - before - after)
        result = smooth + total
        if channel == 1:
            result = jnp.maximum(result, 0.0)
        next_ref[:, channel, :] = result
        if share % 128:
            room = 128 - share % 128
            result = jnp.concatenate([result, jnp.zeros((room, depth), jnp.float32)], axis=0)
        gathered_ref[me, rows, :] = result.T[:, :share].astype(jnp.bfloat16)

    def spread_copy(peer, slot):
        return pltpu.make_async_remote_copy(
            src_ref=gathered_ref.at[slot],
            dst_ref=gathered_ref.at[slot],
            send_sem=spread_sem.at[peer],
            recv_sem=gather_sems.at[slot],
            device_id=(peer, slab),
            device_id_type=MESH,
        )

    @pl.loop(1, groups)
    def _(step):
        spread_copy(lax.rem(me + step, groups), me).start()

    def forward(where, fresh):
        for angle in range(local_angles):
            image = None
            for part in range(per_unit):
                piece = lax.dot_general(
                    gathered_ref[where * per_unit + part],
                    wide_ref[
                        where,
                        angle * detector : (angle + 1) * detector,
                        part * share : (part + 1) * share,
                    ],
                    (((1,), (1,)), ((), ())),
                    preferred_element_type=jnp.float32,
                )
                image = piece if image is None else image + piece
            if fresh:
                projection_ref[angle] = image
            else:
                projection_ref[angle] += image

    def gather_wait(source):
        spread_copy(source, source).wait_recv()

    if per_unit > 1:
        for part in range(per_unit):
            owner = my_unit * per_unit + part

            @pl.when(owner != me)
            def _():
                gather_wait(owner)

    forward(my_unit, True)

    @pl.loop(1, unit_count)
    def _(step):
        where = lax.rem(my_unit + unit_count - step, unit_count)
        for part in range(per_unit):
            gather_wait(where * per_unit + part)
        forward(where, False)

    @pl.loop(1, groups)
    def _(step):
        peer = lax.rem(me + step, groups)
        term_copy(peer).wait_send()
        spread_copy(peer, me).wait_send()


def shards(groups, slabs, updates, interp_tiles, band_start, angle_id, angle_weight, volume):
    local_angles, channels, depth, detector = updates.shape
    tile_count, band_width, block_size = interp_tiles.shape[1:]
    share = volume.shape[0]
    row_count = channels * depth
    unit = max(share, block_size)
    unit_count = tile_count * block_size // unit
    turns = {1: (), 2: (1,)}.get(slabs, (1, slabs - 1))
    slots = max(1, len(turns))
    half = jnp.bfloat16
    vmem = pl.BlockSpec(memory_space=pltpu.VMEM)
    smem = pl.BlockSpec(memory_space=pltpu.SMEM)
    dma = pltpu.SemaphoreType.DMA
    volume_next, projection = pl.pallas_call(
        functools.partial(kernel, groups, slabs, turns),
        name="project",
        out_shape=(
            jax.ShapeDtypeStruct(volume.shape, jnp.float32),
            jax.ShapeDtypeStruct((local_angles, row_count, detector), jnp.float32),
        ),
        in_specs=[smem, smem, smem, vmem, pl.BlockSpec(memory_space=pl.ANY), vmem],
        out_specs=(vmem, vmem),
        scratch_shapes=[
            pltpu.VMEM(interp_tiles.shape, half),
            pltpu.VMEM((unit_count, local_angles * detector, unit), half),
            pltpu.VMEM((row_count, local_angles * detector), half),
            pltpu.VMEM((groups, row_count, share), half),
            pltpu.VMEM((groups, row_count, share), half),
            pltpu.VMEM((groups, row_count, share), half),
            pltpu.VMEM((slots,) + volume.shape, jnp.float32),
            dma((unit_count,)),
            dma((groups,)),
            dma((groups,)),
            dma((groups,)),
            dma((groups,)),
            dma((2, slots)),
        ],
        compiler_params=pltpu.CompilerParams(
            collective_id=0, has_side_effects=True, vmem_limit_bytes=60 * 1024 * 1024
        ),
    )(
        band_start,
        angle_id,
        angle_weight,
        updates.reshape(local_angles, row_count, detector),
        interp_tiles,
        volume,
    )
    return volume_next, projection.reshape(updates.shape)


def solution(mesh):
    placed = (
        P("ang", None, "slab", None),
        P("ang", None, None, None),
        P("ang", None),
        P("ang"),
        P(),
        P("ang", None, "slab"),
    )
    return jax.shard_map(
        functools.partial(shards, mesh.shape["ang"], mesh.shape["slab"]),
        mesh=mesh,
        in_specs=placed,
        out_specs=(P("ang", None, "slab"), P("ang", None, "slab", None)),
        check_vma=False,
    )
```

time: 302 us -> 121 us (0.40)
  the two profiles are of different devices: /device:TPU:0 before, /device:TPU:30 now
where the time goes in v1:
time: 121 us
  Pallas kernels  116 us (96%)
  local copies, waits for them, and re-layouts  4.75 us (4%)
    pallas_call x1, Pallas kernels, shards(): pl.pallas_call(functools.partial(kernel, groups, slabs, turns), name='pro...  116 us
    unnamed x2, local copies, waits for them, and re-layouts  4.75 us

profile of v1, /device:TPU:30, one launch (start us, length us, event | category | flops | bytes accessed | tf_op | source)
XLA Modules:
  0.0 120.9 jit_solution(5385134712035410531)
XLA Ops:
  0.6 115.5 %project.1 = (f32[256,2,128]{2,1,0:T(2,128)}, f32[4,256,512]{2,1,0:T(8,128)}) custom-call(s32[4,32]{1,0:T(4,128)} %starts_ref.1, s32[4]{0:T(128)} %ids_ref.1, f32[64]{0:T(128)} %weights_ref.1, f32[4,256,512]{2,1,0:T(8,128)} %bitcast.3, bf16[4,32,256,128]{3,2,1,0:T(8,128)(2,1)} %tiles_hbm.1, f32[256,2,128]{2,1,0:T(2,128)} %volume_ref.1), custom_call_target="tpu_custom_call" | custom-call | tf_op jit(solution)/shard_map/project/pallas_call | solution.py:279
  116.1 1.7 %copy.10 = f32[256,2,128]{2,1,0:T(2,128)} copy(f32[256,2,128]{2,1,0:T(2,128)} %get-tuple-element.8) | data formatting | bytes 524288
  117.8 3.1 %copy.11 = f32[4,2,128,512]{3,2,1,0:T(8,128)} copy(f32[4,2,128,512]{3,2,1,0:T(8,128)} %bitcast.2) | data formatting | bytes 4194304

commit v2 on v1

--- a/solution.py
+++ b/solution.py
@@ -202,19 +202,27 @@
             result = jnp.concatenate([result, jnp.zeros((room, depth), jnp.float32)], axis=0)
         gathered_ref[me, rows, :] = result.T[:, :share].astype(jnp.bfloat16)
 
-    def spread_copy(peer, slot):
+    inner = 4 if groups % 4 == 0 else 1
+    outer = groups // inner
+    my_outer, my_inner = me // inner, lax.rem(me, inner)
+
+    def device_of(up, along):
+        return lax.rem(my_outer + up, outer) * inner + lax.rem(my_inner + along, inner)
+
+    def spread_copy(peer, slot, ticket):
         return pltpu.make_async_remote_copy(
             src_ref=gathered_ref.at[slot],
             dst_ref=gathered_ref.at[slot],
-            send_sem=spread_sem.at[peer],
+            send_sem=spread_sem.at[ticket],
             recv_sem=gather_sems.at[slot],
             device_id=(peer, slab),
             device_id_type=MESH,
         )
 
-    @pl.loop(1, groups)
-    def _(step):
-        spread_copy(lax.rem(me + step, groups), me).start()
+    for up in range(1, outer):
+        spread_copy(device_of(up, 0), me, up * inner).start()
+    for along in range(1, inner):
+        spread_copy(device_of(0, along), me, along).start()
 
     def forward(where, fresh):
         for angle in range(local_angles):
@@ -236,31 +244,40 @@
             else:
                 projection_ref[angle] += image
 
-    def gather_wait(source):
-        spread_copy(source, source).wait_recv()
+    def arrived(source):
+        spread_copy(source, source, 0).wait_recv()
+
+    if per_unit == 1:
+        forward(me, True)
+
+    for up in range(1, outer):
+        source = device_of(outer - up, 0)
+        arrived(source)
+        for along in range(1, inner):
+            spread_copy(device_of(0, along), source, up * inner + along).start()
+        if per_unit == 1:
+            forward(source, False)
+
+    @pl.loop(0, outer)
+    def _(up):
+        for along in range(1, inner):
+            source = device_of(outer - up, inner - along)
+            arrived(source)
+            if per_unit == 1:
+                forward(source, False)
 
     if per_unit > 1:
-        for part in range(per_unit):
-            owner = my_unit * per_unit + part
-
-            @pl.when(owner != me)
-            def _():
-                gather_wait(owner)
-
-    forward(my_unit, True)
-
-    @pl.loop(1, unit_count)
-    def _(step):
-        where = lax.rem(my_unit + unit_count - step, unit_count)
-        for part in range(per_unit):
-            gather_wait(where * per_unit + part)
-        forward(where, False)
+        forward(0, True)
+
+        @pl.loop(1, unit_count)
+        def _(where):
+            forward(where, False)
 
     @pl.loop(1, groups)
     def _(step):
         peer = lax.rem(me + step, groups)
         term_copy(peer).wait_send()
-        spread_copy(peer, me).wait_send()
+        spread_copy(peer, me, step).wait_send()
 
 
 def shards(groups, slabs, updates, interp_tiles, band_start, angle_id, angle_weight, volume):

time: 121 us -> 98.3 us (0.81)
  the two profiles are of different devices: /device:TPU:30 before, /device:TPU:0 now
where the time goes in v2:
time: 98.3 us; the launch traced here: 96.9 us
  Pallas kernels  91.5 us (93%)
  local copies, waits for them, and re-layouts  4.75 us (5%)
    pallas_call x1, Pallas kernels, shards(): pl.pallas_call(functools.partial(kernel, groups, slabs, turns), name='pro...  91.5 us
    unnamed x2, local copies, waits for them, and re-layouts  4.75 us

profile of v2, /device:TPU:0, one launch (start us, length us, event | category | flops | bytes accessed | tf_op | source)
XLA Modules:
  0.0 96.9 jit_solution(1595645557837612823)
XLA Ops:
  0.6 91.5 %project.1 = (f32[256,2,128]{2,1,0:T(2,128)}, f32[4,256,512]{2,1,0:T(8,128)}) custom-call(s32[4,32]{1,0:T(4,128)} %starts_ref.1, s32[4]{0:T(128)} %ids_ref.1, f32[64]{0:T(128)} %weights_ref.1, f32[4,256,512]{2,1,0:T(8,128)} %bitcast.3, bf16[4,32,256,128]{3,2,1,0:T(8,128)(2,1)} %tiles_hbm.1, f32[256,2,128]{2,1,0:T(2,128)} %volume_ref.1), custom_call_target="tpu_custom_call" | custom-call | tf_op jit(solution)/shard_map/project/pallas_call | solution.py:296
  92.2 1.7 %copy.10 = f32[256,2,128]{2,1,0:T(2,128)} copy(f32[256,2,128]{2,1,0:T(2,128)} %get-tuple-element.8) | data formatting | bytes 524288
  93.8 3.1 %copy.11 = f32[4,2,128,512]{3,2,1,0:T(8,128)} copy(f32[4,2,128,512]{3,2,1,0:T(8,128)} %bitcast.2) | data formatting | bytes 4194304
